TPU v7x, 32 devices: a whole 2x2x4 slice. The times are simulated.
32 devices in a mesh: tile: 8 (over z, x), mem: 4 (over y, core).
Axes of the slice: x: 2, y: 2, z: 4, core: 2. Of those that a mesh axis runs over, the one named last changes fastest.
Arguments:
- footprints: bfloat16 [1024, 128, 128], P('tile'), may hold values from -0.1875 to 0.1875
- tile_row: int32 [1024], P('tile'), may hold values from 0 to 127, as said below
- tile_col: int32 [1024], P('tile'), may hold values from 0 to 63, as said below
- prior_flux: bfloat16 [256, 8192], P('mem', 'tile'), may hold values from -12 to 12
- observed: float32 [256, 16384], P('mem', 'tile'), may hold values from -6 to 6
- precision_weight: int32 [16384], P('tile'), may hold values from 1 to 16
Outputs:
- gradient: float32 [256, 8192], P('mem', 'tile')
Inputs may be any that keep to these rules, and one draw needn't show every extreme that they name: Among the 128 tiles of each index of tile, at most 24 have a row block of one owner (owner = tile_row // 16); in every draw one owner gets exactly 24 from every index. Likewise with owner = tile_col // 8: at most 24 from one index of tile to one owner, and one owner gets exactly 24 from every index.
All inputs are finite; a program needn't handle non-finite values.
Results may differ from a plain program's by a relative error of at most 0.0052.
Values may be sent and summed in bfloat16 or wider, within the bound.
No kernel may reach another device: no remote copies, remote signals or barrier semaphores. Data moves between devices by JAX's collectives and lax.ppermute only.
A program may use at most 64 MiB of HBM per device.

v0:
```python
import jax
import jax.numpy as jnp
from jax import lax
from jax.sharding import PartitionSpec as P

MEMBERS = 256
FLUX_DEV = 8
SOUND_DEV = 16


def slot_of(owners, capacity):
    entries = owners.shape[0]
    position = jnp.arange(entries)
    earlier = (owners[:, None] == owners[None, :]) & (position[None, :] < position[:, None])
    return owners * capacity + jnp.sum(earlier.astype(jnp.int32), axis=1)


def invert(slot_ids, slot_total):
    matches = slot_ids[None, :] == jnp.arange(slot_total)[:, None]
    sources = jnp.sum(jnp.where(matches, jnp.arange(slot_ids.shape[0])[None, :], 0), axis=1)
    return (sources, jnp.any(matches, axis=1))


def to_slots(values, sources, usage_flags):
    placed = jnp.take(values, sources, axis=1)
    return jnp.where(usage_flags[None, :, None], placed, jnp.zeros_like(placed))


def body(footprints, tile_row, tile_col, prior_flux, observed, precision_weight):
    devices_tile = lax.axis_size("tile")
    tile_count = footprints.shape[0]
    tile_size = footprints.shape[1]
    capacity = tile_count // devices_tile + max(1, tile_count // (2 * devices_tile))
    slot_total = devices_tile * capacity
    local_members = prior_flux.shape[0]
    local_sum = jnp.sum(prior_flux.astype(jnp.float32), axis=0)
    ensemble_sum = lax.psum(local_sum, "mem")
    ensemble_mean = ensemble_sum / MEMBERS
    member_deviations = (prior_flux.astype(jnp.float32) - ensemble_mean[None, :]).astype(
        jnp.bfloat16
    )
    row_owner = tile_row // SOUND_DEV
    row_local = tile_row % SOUND_DEV
    row_slot = slot_of(row_owner, capacity)
    row_source, row_used = invert(row_slot, slot_total)
    gathered = lax.all_gather(member_deviations, "tile", axis=1, tiled=True)
    retrieved_blocks = jnp.take(gathered.reshape(local_members, -1, tile_size), tile_col, axis=1)
    forward_terms = jnp.einsum(
        "mtk,trk->mtr", retrieved_blocks, footprints, preferred_element_type=jnp.float32
    )
    row_index = jnp.where(row_used, jnp.take(row_local, row_source), SOUND_DEV)
    sent_terms = to_slots(forward_terms, row_source, row_used)
    got_terms, got_rows = (
        lax.all_to_all(sent_terms, "tile", split_axis=1, concat_axis=1, tiled=True),
        lax.all_to_all(row_index[None, :], "tile", split_axis=1, concat_axis=1, tiled=True),
    )
    got_rows = got_rows[0]
    row_match = (got_rows[None, :] == jnp.arange(SOUND_DEV)[:, None]).astype(jnp.float32)
    modelled = jnp.einsum("ds,msk->mdk", row_match, got_terms, precision=lax.Precision.HIGHEST)
    targets = observed.reshape(local_members, SOUND_DEV, tile_size)
    obs_weight = (precision_weight.astype(jnp.float32) / 8.0).reshape(SOUND_DEV, tile_size)
    weighted = (obs_weight[None, :, :] * (modelled - targets)).astype(jnp.bfloat16)
    reply_rows = jnp.take(weighted, jnp.minimum(got_rows, SOUND_DEV - 1), axis=1)
    returned = lax.all_to_all(reply_rows, "tile", split_axis=1, concat_axis=1, tiled=True)
    residual_tiles = jnp.take(returned, row_slot, axis=1)
    backward_terms = jnp.einsum(
        "mtr,trk->mtk", residual_tiles, footprints, preferred_element_type=jnp.float32
    )
    picked = (tile_col[None, :] == jnp.arange(lax.axis_size("tile") * FLUX_DEV)[:, None]).astype(
        jnp.float32
    )
    reduced_total = lax.psum_scatter(
        jnp.einsum("ct,mtk->cmk", picked, backward_terms, precision=lax.Precision.HIGHEST),
        "tile",
        scatter_dimension=0,
        tiled=True,
    )
    gradient = reduced_total.transpose(1, 0, 2).reshape(local_members, FLUX_DEV * tile_size)
    return gradient


def solution(mesh):
    in_specs = (
        P("tile", None, None),
        P("tile"),
        P("tile"),
        P("mem", "tile"),
        P("mem", "tile"),
        P("tile"),
    )
    out_specs = P("mem", "tile")
    return jax.shard_map(body, mesh=mesh, in_specs=in_specs, out_specs=out_specs, check_vma=False)
```

profile of v0, /device:TPU:0, one launch (start us, length us, event | category | flops | bytes accessed | tf_op | source)
XLA Modules:
  0.0 394.9 jit_solution(9114734959783431947)
XLA Ops:
  6.5 0.9 convert_reduce_fusion
  7.5 8.4 %psum.7 = f32[1024]{0:T(1024)S(1)} all-reduce(f32[1024]{0:T(1024)S(1)} %convert_reduce_fusion), channel_id=1, replica_groups=mesh['tile'=8,'mem'=4] {'mem'}, use_global_device_ids=true, to_apply=%region_4.5 | all-reduce | flops 1024 | bytes 8192 | tf_op jit(solution)/shard_map/psum | solution.py:37
  15.9 1.6 fusion.24
  18.6 1.6 gather_fusion
  21.0 5.8 %all-to-all-start = ((s32[1,8,24]{2,0,1:T(1,128)}), s32[1,8,24]{2,0,1:T(1,128)S(1)}, u32[]{:S(2)}, u32[]{:S(2)}) async-start(s32[1,8,24]{2,0,1:T(1,128)} %bitcast.3), calls=%async_computation | async-start | bytes 8192 | tf_op jit(solution)/shard_map/all_to_all | solution.py:55
  28.2 30.0 %all-gather.2.cloned.1.call-done = bf16[64,8192]{1,0:T(8,128)(2,1)} async-done(((bf16[64,1024]{1,0:T(8,128)(2,1)}), bf16[64,8192]{1,0:T(8,128)(2,1)}) %all-gather.2.cloned.1.call-update) | async-done | bytes 1048592 | tf_op jit(solution)/shard_map/all_gather | solution.py:46
  58.2 1.5 copy_bitcast_fusion
  59.7 1.0 gather_fusion.1
  60.7 7.0 %convolution_bitcast_fusion.1 = f32[64,128,128]{2,0,1:T(8,128)} fusion(bf16[128,128,128]{2,1,0:T(8,128)(2,1)} %param.6, bf16[128,64,128]{2,1,0:T(8,128)(2,1)S(1)} %gather_fusion.1, pred[128]{0:T(512)(128)(4,1)S(1)} %compare_and_fusion), kind=kOutput, calls=%fused_computation.12 | convolution fusion | flops 269484032 | bytes 10485888 | tf_op jit(solution)/shard_map/mtk,trk->mtr/dot_general | solution.py:48
  67.7 5.8 %gather_fusion.2 = f32[192,64,128]{2,1,0:T(8,128)} fusion(f32[64,128,128]{2,0,1:T(8,128)} %convolution_bitcast_fusion.1, s32[1024]{0:T(1024)S(1)} %pad_clamp_fusion.3), kind=kCustom, calls=%fused_computation.2 | custom fusion | bytes 12583680 | tf_op jit(solution)/shard_map/jit(_take)/gather | solution.py:25
  73.5 5.4 %select_bitcast_fusion = f32[64,192,128]{2,0,1:T(8,128)} fusion(f32[192,64,128]{2,1,0:T(8,128)} %gather_fusion.2, pred[192]{0:T(512)(128)(4,1)S(1)} %fusion.25, pred[192]{0:T(512)(128)(4,1)S(1)} %compare_and_fusion.1), kind=kLoop, calls=%fused_computation.7 | loop fusion | flops 3145728 | bytes 12583296 | tf_op jit(solution)/shard_map/jit(_where)/select_n | solution.py:26
  79.0 4.9 %all-to-all-start.1 = ((f32[64,192,128]{2,0,1:T(8,128)}), f32[64,192,128]{2,0,1:T(8,128)}, u32[]{:S(2)}, u32[]{:S(2)}) async-start(f32[64,192,128]{2,0,1:T(8,128)} %select_bitcast_fusion), calls=%async_computation.1 | async-start | bytes 12582912 | tf_op jit(solution)/shard_map/all_to_all | solution.py:54
  84.5 0.7 minimum_reduce_fusion
  85.4 135.2 %all-to-all-done.1 = f32[64,192,128]{2,0,1:T(8,128)} async-done(((f32[64,192,128]{2,0,1:T(8,128)}), f32[64,192,128]{2,0,1:T(8,128)}, u32[]{:S(2)}, u32[]{:S(2)}) %all-to-all-start.1) | async-done | bytes 6291488 | tf_op jit(solution)/shard_map/all_to_all | solution.py:54
  220.6 8.1 %fusion.19 = bf16[64,16,128]{2,1,0:T(8,128)(2,1)S(1)} fusion(f32[64,16,128]{2,1,0:T(8,128)S(1)} %bitcast.49, f32[64,192,128]{2,0,1:T(8,128)} %all-to-all-done.1, f32[16,128]{1,0:T(8,128)S(1)} %multiply_bitcast_fusion, s32[192]{0:T(256)S(1)} %squeeze.3), kind=kOutput, calls=%fused_computation.22 | convolution fusion | flops 302386176 | bytes 7086848 | tf_op jit(solution)/shard_map/ds,msk->mdk/dot_general | solution.py:59
  228.7 1.2 gather_fusion.3
  229.9 2.1 select_bitcast_fusion.1
  232.0 3.6 all-to-all-start.2
  235.7 70.8 %all-to-all-done.2 = bf16[64,192,128]{2,0,1:T(8,128)(2,1)S(1)} async-done(((bf16[64,192,128]{2,0,1:T(8,128)(2,1)}), bf16[64,192,128]{2,0,1:T(8,128)(2,1)S(1)}, u32[]{:S(2)}, u32[]{:S(2)}) %all-to-all-start.2) | async-done | bytes 3145760 | tf_op jit(solution)/shard_map/all_to_all | solution.py:64
  306.5 2.2 gather_fusion.4
  308.7 4.1 %convolution_bitcast_fusion = f32[64,128,128]{2,0,1:T(8,128)S(1)} fusion(bf16[128,128,128]{2,1,0:T(8,128)(2,1)} %param.6, bf16[128,64,128]{2,1,0:T(8,128)(2,1)} %gather_fusion.4, pred[128]{0:T(512)(128)(4,1)S(1)} %get-tuple-element.7), kind=kOutput, calls=%fused_computation.11 | convolution fusion | flops 269484032 | bytes 10485888 | tf_op jit(solution)/shard_map/mtr,trk->mtk/dot_general | solution.py:66
  312.8 5.4 %fusion.2 = f32[64,64,128]{2,0,1:T(8,128)} fusion(f32[64,128,128]{2,0,1:T(8,128)S(1)} %convolution_bitcast_fusion, s32[128]{0:T(128)S(1)} %copy-done.2), kind=kOutput, calls=%fused_computation.8 | convolution fusion | flops 805314560 | bytes 6291968 | tf_op jit(solution)/shard_map/ct,mtk->cmk/dot_general | solution.py:73
  318.3 68.2 %reduce-scatter.2.cloned.1.call-done = f32[8,64,128]{2,0,1:T(8,128)} async-done(((f32[64,64,128]{2,0,1:T(8,128)}), f32[8,64,128]{2,0,1:T(8,128)}) %reduce-scatter.2.cloned.1.call-update) | async-done | bytes 262160 | tf_op jit(solution)/shard_map/reduce_scatter | solution.py:72
  386.4 1.7 copy.42
  (38 shorter events, 4.3 us)
Async XLA Ops:
  6.5 51.7 %all-gather.2.cloned.1.call-start = ((), (), s32[]{:S(2)}) async-start(), calls=%async_computation.4 | async-start | bytes 1179648 | tf_op jit(solution)/shard_map/all_gather | solution.py:46
  21.0 57.9 %all-to-all-start = ((s32[1,8,24]{2,0,1:T(1,128)}), s32[1,8,24]{2,0,1:T(1,128)S(1)}, u32[]{:S(2)}, u32[]{:S(2)}) async-start(s32[1,8,24]{2,0,1:T(1,128)} %bitcast.3), calls=%async_computation | async-start | bytes 8192 | tf_op jit(solution)/shard_map/all_to_all | solution.py:55
  79.0 4.9 %copy-start = (f32[64,2048]{1,0:T(8,128)S(1)}, f32[64,2048]{1,0:T(8,128)}, u32[]{:S(2)}) copy-start(f32[64,2048]{1,0:T(8,128)} %param.10) | copy-start | bytes 1572868
  79.0 5.0 %copy-start.1 = (s32[2048]{0:T(1024)S(1)}, s32[2048]{0:T(1024)}, u32[]{:S(2)}) copy-start(s32[2048]{0:T(1024)} %param.11) | copy-start | bytes 24580
  79.0 141.6 %all-to-all-start.1 = ((f32[64,192,128]{2,0,1:T(8,128)}), f32[64,192,128]{2,0,1:T(8,128)}, u32[]{:S(2)}, u32[]{:S(2)}) async-start(f32[64,192,128]{2,0,1:T(8,128)} %select_bitcast_fusion), calls=%async_computation.1 | async-start | bytes 12582912 | tf_op jit(solution)/shard_map/all_to_all | solution.py:54
  232.0 74.5 %all-to-all-start.2 = ((bf16[64,192,128]{2,0,1:T(8,128)(2,1)}), bf16[64,192,128]{2,0,1:T(8,128)(2,1)S(1)}, u32[]{:S(2)}, u32[]{:S(2)}) async-start(bf16[64,192,128]{2,0,1:T(8,128)(2,1)} %select_bitcast_fusion.1), calls=%async_computation.2 | async-start | bytes 6291456 | tf_op jit(solution)/shard_map/all_to_all | solution.py:64
  235.6 150.8 %reduce-scatter.2.cloned.1.call-start = ((), (), s32[]{:S(2)}) async-start(), calls=%async_computation.5 | async-start | bytes 2359296 | tf_op jit(solution)/shard_map/reduce_scatter | solution.py:72
  308.7 4.1 %copy-start.2 = (s32[128]{0:T(128)S(1)}, s32[128]{0:T(128)}, u32[]{:S(2)}) copy-start(s32[128]{0:T(128)} %param.8) | copy-start | bytes 1540
Sparse Core Ops, SparseCore 0:
  17.6 40.5 all-gather.1
  318.4 67.9 reduce-scatter.1
where the time goes:
time: 396 us; the launch traced here: 395 us
  waiting for transfers between devices  304 us (77%)
  matrix products  24.7 us (6%)
  local copies, waits for them, and re-layouts  15.9 us (4%)
  starting transfers between devices  14.4 us (4%)
  other arithmetic  13.8 us (3%)
  between operations  13.6 us (3%)
  blocking collectives  8.4 us (2%)
    all_to_all x1, waiting for transfers between devices, body(): lax.all_to_all(sent_terms, 'tile', split_axis=1, concat_axis=1, tiled=True)  135 us
    all_to_all x1, waiting for transfers between devices, body(): lax.all_to_all(reply_rows, 'tile', split_axis=1, concat_axis=1, tiled=True)  70.8 us
    reduce_scatter x1, waiting for transfers between devices, body(): lax.psum_scatter(jnp.einsum('ct,mtk->cmk', picked, backward_terms, precis...  68.2 us
    all_gather x1, waiting for transfers between devices, body(): gathered = lax.all_gather(member_deviations, 'tile', axis=1, tiled=True)  30 us
    psum x1, blocking collectives, body(): ensemble_sum = lax.psum(local_sum, 'mem')  8.4 us
    dot_general x1, matrix products, body(): jnp.einsum('ds,msk->mdk', row_match, got_terms, precision=lax.Precision.H...  8.12 us
  transfers between devices with their start and end apart: 5, of which 4 were waited for; matrix products, arithmetic and copies ran while one was open for 7% of the time, Pallas kernels for 0%

commit v1 on v0

--- a/solution.py
+++ b/solution.py
@@ -43,7 +43,7 @@
     row_local = tile_row % SOUND_DEV
     row_slot = slot_of(row_owner, capacity)
     row_source, row_used = invert(row_slot, slot_total)
-    gathered = lax.all_gather(member_deviations, "tile", axis=1, tiled=True)
+    gathered = jnp.concatenate(lax.all_gather(member_deviations, "tile"), axis=1)
     retrieved_blocks = jnp.take(gathered.reshape(local_members, -1, tile_size), tile_col, axis=1)
     forward_terms = jnp.einsum(
         "mtk,trk->mtr", retrieved_blocks, footprints, preferred_element_type=jnp.float32

time: 396 us -> 397 us (level)
  no operation moved by 1% of the time
where the time goes in v1:
time: 397 us
  waiting for transfers between devices  304 us (77%)
  matrix products  24.7 us (6%)
  local copies, waits for them, and re-layouts  17.4 us (4%)
  starting transfers between devices  14.8 us (4%)
  other arithmetic  13.8 us (3%)
  between operations  13.6 us (3%)
  blocking collectives  8.4 us (2%)
    all_to_all x1, waiting for transfers between devices, body(): lax.all_to_all(sent_terms, 'tile', split_axis=1, concat_axis=1, tiled=True)  135 us
    all_to_all x1, waiting for transfers between devices, body(): lax.all_to_all(reply_rows, 'tile', split_axis=1, concat_axis=1, tiled=True)  70.6 us
    reduce_scatter x1, waiting for transfers between devices, body(): lax.psum_scatter(jnp.einsum('ct,mtk->cmk', picked, backward_terms, precis...  68.4 us
    all_gather x1, waiting for transfers between devices, body(): lax.all_gather(member_deviations, 'tile')  30.1 us
    psum x1, blocking collectives, body(): ensemble_sum = lax.psum(local_sum, 'mem')  8.4 us
    dot_general x1, matrix products, body(): jnp.einsum('ds,msk->mdk', row_match, got_terms, precision=lax.Precision.H...  8.12 us
  transfers between devices with their start and end apart: 5, of which 4 were waited for; matrix products, arithmetic and copies ran while one was open for 7% of the time, Pallas kernels for 0%

profile of v1, /device:TPU:0, one launch (start us, length us, event | category | flops | bytes accessed | tf_op | source)
XLA Modules:
  0.0 396.7 jit_solution(2656614828763084823)
XLA Ops:
  6.5 0.9 convert_reduce_fusion
  7.5 8.4 %psum.7 = f32[1024]{0:T(1024)S(1)} all-reduce(f32[1024]{0:T(1024)S(1)} %convert_reduce_fusion), channel_id=1, replica_groups=mesh['tile'=8,'mem'=4] {'mem'}, use_global_device_ids=true, to_apply=%region_4.5 | all-reduce | flops 1024 | bytes 8192 | tf_op jit(solution)/shard_map/psum | solution.py:37
  15.9 1.6 fusion.24
  18.6 1.6 gather_fusion
  21.0 5.8 %all-to-all-start = ((s32[1,8,24]{2,0,1:T(1,128)}), s32[1,8,24]{2,0,1:T(1,128)S(1)}, u32[]{:S(2)}, u32[]{:S(2)}) async-start(s32[1,8,24]{2,0,1:T(1,128)} %bitcast.3), calls=%async_computation | async-start | bytes 8192 | tf_op jit(solution)/shard_map/all_to_all | solution.py:55
  28.2 30.1 %all-gather.3.cloned.1.call-done = bf16[512,1024]{1,0:T(8,128)(2,1)} async-done(((bf16[64,1024]{1,0:T(8,128)(2,1)}), bf16[512,1024]{1,0:T(8,128)(2,1)}) %all-gather.3.cloned.1.call-update) | async-done | bytes 1048592 | tf_op jit(solution)/shard_map/all_gather | solution.py:46
  58.2 1.8 copy.47
  60.5 0.7 copy.27
  61.2 1.0 gather_fusion.1
  62.2 7.0 %convolution_bitcast_fusion.1 = f32[64,128,128]{2,0,1:T(8,128)} fusion(bf16[128,128,128]{2,1,0:T(8,128)(2,1)} %param.6, bf16[128,64,128]{2,1,0:T(8,128)(2,1)S(1)} %gather_fusion.1, pred[128]{0:T(512)(128)(4,1)S(1)} %compare_and_fusion), kind=kOutput, calls=%fused_computation.12 | convolution fusion | flops 269484032 | bytes 10485888 | tf_op jit(solution)/shard_map/mtk,trk->mtr/dot_general | solution.py:48
  69.2 5.8 %gather_fusion.2 = f32[192,64,128]{2,1,0:T(8,128)} fusion(f32[64,128,128]{2,0,1:T(8,128)} %convolution_bitcast_fusion.1, s32[1024]{0:T(1024)S(1)} %pad_clamp_fusion.3), kind=kCustom, calls=%fused_computation.2 | custom fusion | bytes 12583680 | tf_op jit(solution)/shard_map/jit(_take)/gather | solution.py:25
  75.0 5.4 %select_bitcast_fusion = f32[64,192,128]{2,0,1:T(8,128)} fusion(f32[192,64,128]{2,1,0:T(8,128)} %gather_fusion.2, pred[192]{0:T(512)(128)(4,1)S(1)} %fusion.25, pred[192]{0:T(512)(128)(4,1)S(1)} %compare_and_fusion.1), kind=kLoop, calls=%fused_computation.7 | loop fusion | flops 3145728 | bytes 12583296 | tf_op jit(solution)/shard_map/jit(_where)/select_n | solution.py:26
  80.5 5.1 %all-to-all-start.1 = ((f32[64,192,128]{2,0,1:T(8,128)}), f32[64,192,128]{2,0,1:T(8,128)}, u32[]{:S(2)}, u32[]{:S(2)}) async-start(f32[64,192,128]{2,0,1:T(8,128)} %select_bitcast_fusion), calls=%async_computation.1 | async-start | bytes 12582912 | tf_op jit(solution)/shard_map/all_to_all | solution.py:54
  87.1 135.0 %all-to-all-done.1 = f32[64,192,128]{2,0,1:T(8,128)} async-done(((f32[64,192,128]{2,0,1:T(8,128)}), f32[64,192,128]{2,0,1:T(8,128)}, u32[]{:S(2)}, u32[]{:S(2)}) %all-to-all-start.1) | async-done | bytes 6291488 | tf_op jit(solution)/shard_map/all_to_all | solution.py:54
  222.1 8.1 %fusion.19 = bf16[64,16,128]{2,1,0:T(8,128)(2,1)S(1)} fusion(f32[64,16,128]{2,1,0:T(8,128)S(1)} %bitcast.49, f32[64,192,128]{2,0,1:T(8,128)} %all-to-all-done.1, f32[16,128]{1,0:T(8,128)S(1)} %multiply_bitcast_fusion, s32[192]{0:T(256)S(1)} %squeeze.3), kind=kOutput, calls=%fused_computation.22 | convolution fusion | flops 302386176 | bytes 7086848 | tf_op jit(solution)/shard_map/ds,msk->mdk/dot_general | solution.py:59
  230.2 1.2 gather_fusion.3
  231.4 2.1 select_bitcast_fusion.1
  233.5 3.6 all-to-all-start.2
  237.4 70.6 %all-to-all-done.2 = bf16[64,192,128]{2,0,1:T(8,128)(2,1)S(1)} async-done(((bf16[64,192,128]{2,0,1:T(8,128)(2,1)}), bf16[64,192,128]{2,0,1:T(8,128)(2,1)S(1)}, u32[]{:S(2)}, u32[]{:S(2)}) %all-to-all-start.2) | async-done | bytes 3145760 | tf_op jit(solution)/shard_map/all_to_all | solution.py:64
  308.0 2.2 gather_fusion.4
  310.2 4.1 %convolution_bitcast_fusion = f32[64,128,128]{2,0,1:T(8,128)S(1)} fusion(bf16[128,128,128]{2,1,0:T(8,128)(2,1)} %param.6, bf16[128,64,128]{2,1,0:T(8,128)(2,1)} %gather_fusion.4, pred[128]{0:T(512)(128)(4,1)S(1)} %get-tuple-element.7), kind=kOutput, calls=%fused_computation.11 | convolution fusion | flops 269484032 | bytes 10485888 | tf_op jit(solution)/shard_map/mtr,trk->mtk/dot_general | solution.py:66
  314.3 5.4 %fusion.2 = f32[64,64,128]{2,0,1:T(8,128)} fusion(f32[64,128,128]{2,0,1:T(8,128)S(1)} %convolution_bitcast_fusion, s32[128]{0:T(128)S(1)} %copy-done.2), kind=kOutput, calls=%fused_computation.8 | convolution fusion | flops 805314560 | bytes 6291968 | tf_op jit(solution)/shard_map/ct,mtk->cmk/dot_general | solution.py:73
  319.8 68.4 %reduce-scatter.2.cloned.1.call-done = f32[8,64,128]{2,0,1:T(8,128)} async-done(((f32[64,64,128]{2,0,1:T(8,128)}), f32[8,64,128]{2,0,1:T(8,128)}) %reduce-scatter.2.cloned.1.call-update) | async-done | bytes 262160 | tf_op jit(solution)/shard_map/reduce_scatter | solution.py:72
  388.2 1.7 copy.48
  (40 shorter events, 5.6 us)
Async XLA Ops:
  6.5 51.7 %all-gather.3.cloned.1.call-start = ((), (), s32[]{:S(2)}) async-start(), calls=%async_computation.5 | async-start | bytes 1179648 | tf_op jit(solution)/shard_map/all_gather | solution.py:46
  21.0 59.4 %all-to-all-start = ((s32[1,8,24]{2,0,1:T(1,128)}), s32[1,8,24]{2,0,1:T(1,128)S(1)}, u32[]{:S(2)}, u32[]{:S(2)}) async-start(s32[1,8,24]{2,0,1:T(1,128)} %bitcast.3), calls=%async_computation | async-start | bytes 8192 | tf_op jit(solution)/shard_map/all_to_all | solution.py:55
  80.5 5.1 %copy-start = (f32[64,2048]{1,0:T(8,128)S(1)}, f32[64,2048]{1,0:T(8,128)}, u32[]{:S(2)}) copy-start(f32[64,2048]{1,0:T(8,128)} %param.10) | copy-start | bytes 1572868
  80.5 5.2 %copy-start.1 = (s32[2048]{0:T(1024)S(1)}, s32[2048]{0:T(1024)}, u32[]{:S(2)}) copy-start(s32[2048]{0:T(1024)} %param.11) | copy-start | bytes 24580
  80.5 141.6 %all-to-all-start.1 = ((f32[64,192,128]{2,0,1:T(8,128)}), f32[64,192,128]{2,0,1:T(8,128)}, u32[]{:S(2)}, u32[]{:S(2)}) async-start(f32[64,192,128]{2,0,1:T(8,128)} %select_bitcast_fusion), calls=%async_computation.1 | async-start | bytes 12582912 | tf_op jit(solution)/shard_map/all_to_all | solution.py:54
  233.5 74.5 %all-to-all-start.2 = ((bf16[64,192,128]{2,0,1:T(8,128)(2,1)}), bf16[64,192,128]{2,0,1:T(8,128)(2,1)S(1)}, u32[]{:S(2)}, u32[]{:S(2)}) async-start(bf16[64,192,128]{2,0,1:T(8,128)(2,1)} %select_bitcast_fusion.1), calls=%async_computation.2 | async-start | bytes 6291456 | tf_op jit(solution)/shard_map/all_to_all | solution.py:64
  237.1 151.0 %reduce-scatter.2.cloned.1.call-start = ((), (), s32[]{:S(2)}) async-start(), calls=%async_computation.4 | async-start | bytes 2359296 | tf_op jit(solution)/shard_map/reduce_scatter | solution.py:72
  310.2 4.1 %copy-start.2 = (s32[128]{0:T(128)S(1)}, s32[128]{0:T(128)}, u32[]{:S(2)}) copy-start(s32[128]{0:T(128)} %param.8) | copy-start | bytes 1540
Sparse Core Ops, SparseCore 0:
  17.6 40.5 all-gather.2
  319.9 68.2 reduce-scatter.1
